TPU v7x, 32 devices: a whole 2x2x4 slice. The times are simulated.
32 devices in a mesh: tp: 2 (over x), dp: 4 (over y, core), rep: 4 (over z).
Axes of the slice: x: 2, y: 2, z: 4, core: 2. Of those that a mesh axis runs over, the one named last changes fastest.
Arguments:
- prompts: bfloat16 [12288, 8192], P(('dp', 'rep'), 'tp'), may hold values from -6 to 6
- frozen_projection_weight: bfloat16 [2, 8192, 2048], P(None, ('dp', 'rep'), 'tp'), may hold values from -5 to 5
- lowrank_down_factor: bfloat16 [2, 8192, 64], P(None, ('dp', 'rep')), may hold values from -0.119628906 to 0.119628906
- lowrank_up_factor: bfloat16 [2, 64, 2048], P(None, None, 'tp'), may hold values from -0.59765625 to 0.59765625
- magnitude: float32 [2, 2048], P(None, 'tp'), may hold values from 0.5 to 2
Outputs:
- key_values: bfloat16 [2, 12288, 2048], P(None, ('dp', 'rep'), 'tp')
All inputs are finite; a program needn't handle non-finite values.
Results may differ from a plain program's by a relative error of at most 0.0049.
Values may be sent and summed in bfloat16 or wider, within the bound.
A program may use at most 128 MiB of HBM per device.

v0:
```python
import jax
import jax.numpy as jnp
from jax import lax
from jax.sharding import PartitionSpec as P

epsilon = 1e-06


def combine_weight_rows(weight_rows, down_rows, up_matrix):
    return weight_rows.astype(jnp.float32) + jnp.dot(
        down_rows, up_matrix, preferred_element_type=jnp.float32
    )


def prefilled_shard_values(
    frozen_projection_weight, lowrank_down_factor, lowrank_up_factor, magnitude, current_layer_index
):
    combined_weight = combine_weight_rows(
        frozen_projection_weight[current_layer_index],
        lowrank_down_factor[current_layer_index],
        lowrank_up_factor[current_layer_index],
    )
    squares = lax.psum(jnp.sum(combined_weight * combined_weight, axis=0), ("dp", "rep"))
    factor = magnitude[current_layer_index] / jnp.sqrt(squares + epsilon)
    return (combined_weight * factor).astype(jnp.bfloat16)


def local(prompts, frozen_projection_weight, lowrank_down_factor, lowrank_up_factor, magnitude):
    layer_total = frozen_projection_weight.shape[0]
    features = lax.all_gather(prompts, "tp", axis=1, tiled=True)
    outputs = []
    for current_layer_index in range(layer_total):
        prefilled_key_values = prefilled_shard_values(
            frozen_projection_weight,
            lowrank_down_factor,
            lowrank_up_factor,
            magnitude,
            current_layer_index,
        )
        result = jnp.dot(
            features,
            lax.all_gather(prefilled_key_values, ("dp", "rep"), axis=0, tiled=True),
            preferred_element_type=jnp.float32,
        )
        outputs.append(result.astype(jnp.bfloat16))
    return jnp.stack(outputs)


def solution(mesh):
    in_specs = (
        P(("dp", "rep"), "tp"),
        P(None, ("dp", "rep"), "tp"),
        P(None, ("dp", "rep"), None),
        P(None, None, "tp"),
        P(None, "tp"),
    )
    out_specs = P(None, ("dp", "rep"), "tp")
    return jax.shard_map(local, mesh=mesh, in_specs=in_specs, out_specs=out_specs, check_vma=False)
```

profile of v0, /device:TPU:0, one launch (start us, length us, event | category | flops | bytes accessed | tf_op | source)
XLA Modules:
  0.0 448.4 jit_solution(12562199270056117100)
XLA Ops:
  6.5 0.0 copy-start.2
  6.5 0.0 copy-start.3
  6.5 0.0 all-gather.6.cloned.1.call-start
  6.5 0.7 all-gather.6.cloned.1.call-update
  7.3 0.0 all-gather.4.cloned.1.call-start
  7.3 0.2 copy-done.2
  7.5 0.0 copy-done.3
  7.5 0.0 copy-start
  7.5 1.8 multiply_reduce_fusion
  9.4 0.1 copy-done
  9.4 0.0 copy-start.4
  9.4 1.8 multiply_reduce_fusion.1
  11.2 35.9 %all-reduce = (f32[1024]{0:T(1024)S(1)}, f32[1024]{0:T(1024)S(1)}) all-reduce(f32[1024]{0:T(1024)S(1)} %get-tuple-element.9, f32[1024]{0:T(1024)S(1)} %get-tuple-element.11), channel_id=1, replica_groups=mesh['tp'=2,'dp'=4,'rep'=4] {'dp','rep'}, use_global_device_ids=true, to_apply=%region_3.0 | all-reduce | flops 2048 | bytes 16384 | tf_op jit(solution)/shard_map/psum | solution.py:23
  47.2 0.0 copy-done.4
  47.2 2.8 multiply_convert_fusion.1
  50.0 0.0 all-gather.4.cloned.1.call-update
  50.1 0.0 all-gather.8.cloned.1.call-start
  50.1 1.2 multiply_convert_fusion
  51.4 0.0 all-gather.8.cloned.1.call-update
  51.4 112.8 %all-gather.6.cloned.1.call-done = bf16[768,8192]{1,0:T(8,128)(2,1)} async-done(((bf16[768,4096]{1,0:T(8,128)(2,1)}), bf16[768,8192]{1,0:T(8,128)(2,1)}) %all-gather.6.cloned.1.call-update) | async-done | bytes 12582928 | tf_op jit(solution)/shard_map/all_gather | solution.py:30
  164.1 128.7 %all-gather.4.cloned.1.call-done = bf16[8192,1024]{1,0:T(8,128)(2,1)} async-done(((bf16[512,1024]{1,0:T(8,128)(2,1)}), bf16[8192,1024]{1,0:T(8,128)(2,1)}) %all-gather.4.cloned.1.call-update) | async-done | bytes 16777232 | tf_op jit(solution)/shard_map/all_gather | solution.py:42
  292.8 20.0 %fusion = bf16[1,768,1024]{1,2,0:T(8,128)(2,1)} fusion(bf16[8192,1024]{1,0:T(8,128)(2,1)} %all-gather.4.cloned.1.call-done, bf16[768,8192]{1,0:T(8,128)(2,1)} %all-gather.6.cloned.1.call-done), kind=kOutput, calls=%fused_computation.9 | convolution fusion | flops 12885688320 | bytes 30932992 | tf_op jit(solution)/shard_map/dot_general | solution.py:40
  312.8 106.8 %all-gather.8.cloned.1.call-done = bf16[8192,1024]{1,0:T(8,128)(2,1)} async-done(((bf16[512,1024]{1,0:T(8,128)(2,1)}), bf16[8192,1024]{1,0:T(8,128)(2,1)}) %all-gather.8.cloned.1.call-update) | async-done | bytes 16777232 | tf_op jit(solution)/shard_map/all_gather | solution.py:42
  419.7 0.0 copy-start.1
  419.7 19.0 %fusion.1 = bf16[1,768,1024]{1,2,0:T(8,128)(2,1)S(1)} fusion(bf16[8192,1024]{1,0:T(8,128)(2,1)} %all-gather.8.cloned.1.call-done, bf16[768,8192]{1,0:T(8,128)(2,1)} %all-gather.6.cloned.1.call-done), kind=kOutput, calls=%fused_computation.10 | convolution fusion | flops 12885688320 | bytes 30932992 | tf_op jit(solution)/shard_map/dot_general | solution.py:40
  438.7 0.0 copy-done.1
  438.7 0.3 pad_maximum_fusion
  439.0 2.9 copy.6
  (3 shorter events, 0.0 us)
Async XLA Ops:
  6.5 0.9 copy-start.2
  6.5 1.0 copy-start.3
  6.5 157.6 %all-gather.6.cloned.1.call-start = ((), (), s32[]{:S(2)}) async-start(), calls=%async_computation.1 | async-start | bytes 18874368 | tf_op jit(solution)/shard_map/all_gather | solution.py:30
  7.3 285.6 %all-gather.4.cloned.1.call-start = ((), (), s32[]{:S(2)}) async-start(), calls=%async_computation | async-start | bytes 17825792 | tf_op jit(solution)/shard_map/all_gather | solution.py:42
  7.5 1.9 copy-start
  9.4 37.7 %copy-start.4 = (f32[2,1024]{1,0:T(2,128)S(1)}, f32[2,1024]{1,0:T(2,128)}, u32[]{:S(2)}) copy-start(f32[2,1024]{1,0:T(2,128)} %param.9) | copy-start | bytes 24580
  50.1 369.6 %all-gather.8.cloned.1.call-start = ((), (), s32[]{:S(2)}) async-start(), calls=%async_computation.2 | async-start | bytes 17825792 | tf_op jit(solution)/shard_map/all_gather | solution.py:42
  419.7 19.0 %copy-start.1 = (bf16[1,768,1024]{1,2,0:T(8,128)(2,1)S(1)}, bf16[1,768,1024]{1,2,0:T(8,128)(2,1)}, u32[]{:S(2)}) copy-start(bf16[1,768,1024]{1,2,0:T(8,128)(2,1)} %fusion) | copy-start | bytes 4718596
Sparse Core Ops, SparseCore 0:
  8.9 155.2 all-gather.5
  166.4 126.4 all-gather.3
  295.0 124.5 all-gather.7
where the time goes:
time: 449 us; the launch traced here: 448 us
  waiting for transfers between devices  349 us (78%)
  matrix products  42.7 us (10%)
  blocking collectives  35.9 us (8%)
  between operations  13.2 us (3%)
    all_gather x2, waiting for transfers between devices, local(): lax.all_gather(prefilled_key_values, ('dp', 'rep'), axis=0, tiled=True)  235 us
    all_gather x1, waiting for transfers between devices, local(): features = lax.all_gather(prompts, 'tp', axis=1, tiled=True)  113 us
    dot_general x2, matrix products, local(): jnp.dot(features, lax.all_gather(prefilled_key_values, ('dp', 'rep'), axi...  39 us
    psum x1, blocking collectives, prefilled_shard_values(): lax.psum(jnp.sum(combined_weight * combined_weight, axis=0), ('dp', 'rep'))  35.9 us
  transfers between devices with their start and end apart: 3, of which 3 were waited for; matrix products, arithmetic and copies ran while one was open for 6% of the time, Pallas kernels for 0%

commit v1 on v0

--- a/solution.py
+++ b/solution.py
@@ -4,6 +4,12 @@
 from jax.sharding import PartitionSpec as P
 
 epsilon = 1e-06
+
+
+def write_the_case(incoming_x, device_axis, axis_no):
+    answer = jnp.stack(lax.axis_size(device_axis) * [incoming_x])
+    tall = lax.all_to_all(answer, device_axis, 0, 0)
+    return jnp.concatenate(tall, axis=axis_no)
 
 
 def combine_weight_rows(weight_rows, down_rows, up_matrix):
@@ -27,7 +33,7 @@
 
 def local(prompts, frozen_projection_weight, lowrank_down_factor, lowrank_up_factor, magnitude):
     layer_total = frozen_projection_weight.shape[0]
-    features = lax.all_gather(prompts, "tp", axis=1, tiled=True)
+    features = write_the_case(prompts, "tp", 1)
     outputs = []
     for current_layer_index in range(layer_total):
         prefilled_key_values = prefilled_shard_values(

time: 449 us -> 327 us (0.73)
  waiting for transfers between devices: 349 us -> 76 us
  blocking collectives: 35.9 us -> 176 us
  other arithmetic: 4.38 us -> 12.7 us
  local copies, waits for them, and re-layouts: 3.15 us -> 8.75 us
    all_gather x2, waiting for transfers between devices: 235 us -> 76 us  [local(): lax.all_gather(prefilled_key_values, ('dp', 'rep'), axis=0, tiled=True)]
    all_to_all x0 -> x1, blocking collectives: none -> 140 us  [write_the_case(): tall = lax.all_to_all(answer, device_axis, 0, 0)]
    all_gather x1 -> x0, waiting for transfers between devices: 113 us -> none  [local(): features = lax.all_gather(prompts, 'tp', axis=1, tiled=True)]
    unnamed x10 -> x9, local copies, waits for them, and re-layouts: 0.27 us -> 8.75 us
    another operation x0 -> x1, other arithmetic: none -> 6.67 us  [write_the_case(): answer = jnp.stack(lax.axis_size(device_axis) * [incoming_x])]
  transfers between devices with their start and end apart: 3 -> 2, of which waited for: 3 -> 1; matrix products, arithmetic and copies ran while one was open for 6% -> 11% of each run, Pallas kernels for 0% -> 0%
where the time goes in v1:
time: 327 us
  blocking collectives  176 us (54%)
  waiting for transfers between devices  76 us (23%)
  matrix products  40.3 us (12%)
  between operations  13.5 us (4%)
  other arithmetic  12.7 us (4%)
  local copies, waits for them, and re-layouts  8.75 us (3%)
    all_to_all x1, blocking collectives, write_the_case(): tall = lax.all_to_all(answer, device_axis, 0, 0)  140 us
    all_gather x2, waiting for transfers between devices, local(): lax.all_gather(prefilled_key_values, ('dp', 'rep'), axis=0, tiled=True)  76 us
    dot_general x2, matrix products, local(): jnp.dot(features, lax.all_gather(prefilled_key_values, ('dp', 'rep'), axi...  36.5 us
    psum x1, blocking collectives, prefilled_shard_values(): lax.psum(jnp.sum(combined_weight * combined_weight, axis=0), ('dp', 'rep'))  36 us
    unnamed x9, local copies, waits for them, and re-layouts  8.75 us
    another operation x1, other arithmetic, write_the_case(): answer = jnp.stack(lax.axis_size(device_axis) * [incoming_x])  6.67 us
  transfers between devices with their start and end apart: 2, of which 1 were waited for; matrix products, arithmetic and copies ran while one was open for 11% of the time, Pallas kernels for 0%

profile of v1, /device:TPU:0, one launch (start us, length us, event | category | flops | bytes accessed | tf_op | source)
XLA Modules:
  0.0 326.8 jit_solution(6724172361121895028)
XLA Ops:
  6.5 0.0 copy-start.1
  6.5 0.0 copy-start.2
  6.5 0.0 copy-start.3
  6.5 0.0 all-gather.5.cloned.1.call-start
  6.5 0.0 copy-start
  6.5 3.3 multiply_reduce_fusion
  9.8 0.0 copy-done.1
  9.8 0.0 copy-done.2
  9.8 0.0 copy-done
  9.8 0.5 multiply_reduce_fusion.1
  10.3 0.0 copy-done.3
  10.3 36.0 %all-reduce = (f32[1024]{0:T(1024)S(1)}, f32[1024]{0:T(1024)S(1)}) all-reduce(f32[1024]{0:T(1024)S(1)} %get-tuple-element.9, f32[1024]{0:T(1024)S(1)} %get-tuple-element.11), channel_id=1, replica_groups=mesh['tp'=2,'dp'=4,'rep'=4] {'dp','rep'}, use_global_device_ids=true, to_apply=%region_3.0 | all-reduce | flops 2048 | bytes 16384 | tf_op jit(solution)/shard_map/psum | solution.py:29
  46.3 2.8 multiply_convert_fusion
  49.1 0.0 all-gather.5.cloned.1.call-update
  49.2 0.0 all-gather.3.cloned.1.call-start
  49.2 1.2 multiply_convert_fusion.1
  50.5 0.0 all-gather.3.cloned.1.call-update
  50.5 8.7 %copy.6 = bf16[768,4096]{0,1:T(8,128)(2,1)} copy(bf16[768,4096]{1,0:T(8,128)(2,1)} %param.5) | data formatting | bytes 12582912 | tf_op args[0]
  59.2 6.7 %pad_maximum_fusion = bf16[2,768,4096]{1,2,0:T(8,128)(2,1)S(1)} fusion(bf16[1,768,4096]{1,2,0:T(8,128)(2,1)} %bitcast.40), kind=kLoop, calls=%fused_computation | loop fusion | flops 6291456 | bytes 18874368 | tf_op jit(solution)/shard_map/stack | solution.py:10
  65.9 139.6 %all_to_all.5 = bf16[2,768,4096]{1,2,0:T(8,128)(2,1)} all-to-all(bf16[2,768,4096]{1,2,0:T(8,128)(2,1)S(1)} %pad_maximum_fusion), channel_id=1, replica_groups=mesh['tp'=2,'dp'=4,'rep'=4] {'tp'}, dimensions={0} | all-to-all | bytes 25165824 | tf_op jit(solution)/shard_map/all_to_all | solution.py:11
  205.5 0.0 all-gather.5.cloned.1.call-done
  205.5 18.3 %fusion.1 = bf16[1,768,1024]{2,1,0:T(8,128)(2,1)S(1)} fusion(bf16[768,8192]{0,1:T(8,128)(2,1)} %bitcast.41, bf16[8192,1024]{1,0:T(8,128)(2,1)} %all-gather.5.cloned.1.call-done), kind=kOutput, calls=%fused_computation.11 | convolution fusion | flops 12885688320 | bytes 30932992 | tf_op jit(solution)/shard_map/dot_general | solution.py:46
  223.8 76.0 %all-gather.3.cloned.1.call-done = bf16[8192,1024]{1,0:T(8,128)(2,1)} async-done(((bf16[512,1024]{1,0:T(8,128)(2,1)}), bf16[8192,1024]{1,0:T(8,128)(2,1)}) %all-gather.3.cloned.1.call-update) | async-done | bytes 16777232 | tf_op jit(solution)/shard_map/all_gather | solution.py:48
  299.7 18.2 %fusion = bf16[1,768,1024]{2,1,0:T(8,128)(2,1)S(1)} fusion(bf16[768,8192]{0,1:T(8,128)(2,1)} %bitcast.42, bf16[8192,1024]{1,0:T(8,128)(2,1)} %all-gather.3.cloned.1.call-done), kind=kOutput, calls=%fused_computation.10 | convolution fusion | flops 12885688320 | bytes 30932992 | tf_op jit(solution)/shard_map/dot_general | solution.py:46
  318.0 1.9 pad_maximum_fusion.1
  (3 shorter events, 0.0 us)
Async XLA Ops:
  6.5 3.3 %copy-start.1 = (bf16[2,64,1024]{2,1,0:T(8,128)(2,1)S(1)}, bf16[2,64,1024]{2,1,0:T(8,128)(2,1)}, u32[]{:S(2)}) copy-start(bf16[2,64,1024]{2,1,0:T(8,128)(2,1)} %param.8) | copy-start | bytes 786436
  6.5 3.3 %copy-start.2 = (bf16[2,512,64]{1,2,0:T(8,128)(2,1)S(1)}, bf16[2,512,64]{1,2,0:T(8,128)(2,1)}, u32[]{:S(2)}) copy-start(bf16[2,512,64]{1,2,0:T(8,128)(2,1)} %param.7) | copy-start | bytes 393220
  6.5 3.8 %copy-start.3 = (f32[2,1024]{1,0:T(2,128)S(1)}, f32[2,1024]{1,0:T(2,128)}, u32[]{:S(2)}) copy-start(f32[2,1024]{1,0:T(2,128)} %param.9) | copy-start | bytes 24580
  6.5 199.0 %all-gather.5.cloned.1.call-start = ((), (), s32[]{:S(2)}) async-start(), calls=%async_computation.2 | async-start | bytes 17825792 | tf_op jit(solution)/shard_map/all_gather | solution.py:48
  6.5 3.3 %copy-start = (bf16[2,512,1024]{2,1,0:T(8,128)(2,1)S(1)}, bf16[2,512,1024]{2,1,0:T(8,128)(2,1)}, u32[]{:S(2)}) copy-start(bf16[2,512,1024]{2,1,0:T(8,128)(2,1)} %param.6) | copy-start | bytes 6291460
  49.2 250.6 %all-gather.3.cloned.1.call-start = ((), (), s32[]{:S(2)}) async-start(), calls=%async_computation.1 | async-start | bytes 17825792 | tf_op jit(solution)/shard_map/all_gather | solution.py:48
Sparse Core Ops, SparseCore 0:
  49.3 123.5 all-gather.4
  175.1 124.5 all-gather.2

commit v2 on v0

--- a/solution.py
+++ b/solution.py
@@ -4,6 +4,11 @@
 from jax.sharding import PartitionSpec as P
 
 epsilon = 1e-06
+
+
+def all_by_exchange(block, mesh_axis, dim):
+    sent = jnp.stack([block] * lax.axis_size(mesh_axis))
+    return jnp.concatenate(lax.all_to_all(sent, mesh_axis, 0, 0), axis=dim)
 
 
 def combine_weight_rows(weight_rows, down_rows, up_matrix):
@@ -39,7 +44,7 @@
         )
         result = jnp.dot(
             features,
-            lax.all_gather(prefilled_key_values, ("dp", "rep"), axis=0, tiled=True),
+            all_by_exchange(prefilled_key_values, ("dp", "rep"), 0),
             preferred_element_type=jnp.float32,
         )
         outputs.append(result.astype(jnp.bfloat16))

time: 449 us -> 828 us (1.84)
  waiting for transfers between devices: 349 us -> 708 us
  local copies, waits for them, and re-layouts: 3.15 us -> 14.8 us
  starting transfers between devices: 0.08 us -> 10.3 us
    all_to_all x0 -> x2, waiting for transfers between devices: none -> 552 us  [all_by_exchange(): return jnp.concatenate(lax.all_to_all(sent, mesh_axis, 0, 0), axis=dim)]
    all_gather x2 -> x0, waiting for transfers between devices: 235 us -> none  [local(): lax.all_gather(prefilled_key_values, ('dp', 'rep'), axis=0, tiled=True)]
    all_gather x1, waiting for transfers between devices: 113 us -> 155 us  [local(): features = lax.all_gather(prompts, 'tp', axis=1, tiled=True)]
    another operation x0 -> x2, local copies, waits for them, and re-layouts: none -> 11.9 us  [all_by_exchange(): sent = jnp.stack([block] * lax.axis_size(mesh_axis))]
    all_to_all x0 -> x2, starting transfers between devices: none -> 10.3 us  [all_by_exchange(): return jnp.concatenate(lax.all_to_all(sent, mesh_axis, 0, 0), axis=dim)]
  transfers between devices with their start and end apart: 3 -> 3, of which waited for: 3 -> 3; matrix products, arithmetic and copies ran while one was open for 6% -> 2% of each run, Pallas kernels for 0% -> 0%
where the time goes in v2:
time: 828 us; the launch traced here: 827 us
  waiting for transfers between devices  708 us (86%)
  matrix products  42.8 us (5%)
  blocking collectives  36 us (4%)
  local copies, waits for them, and re-layouts  14.8 us (2%)
  between operations  13.5 us (2%)
  starting transfers between devices  10.3 us (1%)
    all_to_all x2, waiting for transfers between devices, all_by_exchange(): return jnp.concatenate(lax.all_to_all(sent, mesh_axis, 0, 0), axis=dim)  552 us
    all_gather x1, waiting for transfers between devices, local(): features = lax.all_gather(prompts, 'tp', axis=1, tiled=True)  155 us
    dot_general x2, matrix products, local(): jnp.dot(features, all_by_exchange(prefilled_key_values, ('dp', 'rep'), 0)...  39 us
    psum x1, blocking collectives, prefilled_shard_values(): lax.psum(jnp.sum(combined_weight * combined_weight, axis=0), ('dp', 'rep'))  36 us
  transfers between devices with their start and end apart: 3, of which 3 were waited for; matrix products, arithmetic and copies ran while one was open for 2% of the time, Pallas kernels for 0%

profile of v2, /device:TPU:0, one launch (start us, length us, event | category | flops | bytes accessed | tf_op | source)
XLA Modules:
  0.0 827.3 jit_solution(9007918507034801088)
XLA Ops:
  6.5 0.0 copy-start.2
  6.5 0.0 copy-start.3
  6.5 0.0 copy-start
  6.5 0.0 copy-start.4
  6.5 3.3 multiply_reduce_fusion
  9.8 0.0 copy-done.2
  9.8 0.0 copy-done.3
  9.8 0.0 copy-done
  9.8 0.5 multiply_reduce_fusion.1
  10.3 0.0 copy-done.4
  10.3 36.0 %all-reduce = (f32[1024]{0:T(1024)S(1)}, f32[1024]{0:T(1024)S(1)}) all-reduce(f32[1024]{0:T(1024)S(1)} %get-tuple-element.9, f32[1024]{0:T(1024)S(1)} %get-tuple-element.11), channel_id=1, replica_groups=mesh['tp'=2,'dp'=4,'rep'=4] {'dp','rep'}, use_global_device_ids=true, to_apply=%region_3.0 | all-reduce | flops 2048 | bytes 16384 | tf_op jit(solution)/shard_map/psum | solution.py:28
  46.3 1.8 multiply_convert_fusion
  48.2 6.0 stack.12
  54.2 5.1 all-to-all-start.1
  59.3 0.2 multiply_convert_fusion.1
  59.6 363.7 %all-to-all-done.1 = bf16[16,512,1024]{2,1,0:T(8,128)(2,1)} async-done(((bf16[16,512,1024]{2,1,0:T(8,128)(2,1)}), bf16[16,512,1024]{2,1,0:T(8,128)(2,1)}, u32[]{:S(2)}, u32[]{:S(2)}) %all-to-all-start.1) | async-done | bytes 16777248 | tf_op jit(solution)/shard_map/all_to_all | solution.py:11
  423.2 5.9 stack.10
  429.2 5.1 all-to-all-start
  434.3 0.0 all-gather.2.cloned.1.call-start
  434.4 0.7 all-gather.2.cloned.1.call-update
  435.1 155.2 %all-gather.2.cloned.1.call-done = bf16[768,8192]{1,0:T(8,128)(2,1)} async-done(((bf16[768,4096]{1,0:T(8,128)(2,1)}), bf16[768,8192]{1,0:T(8,128)(2,1)}) %all-gather.2.cloned.1.call-update) | async-done | bytes 12582928 | tf_op jit(solution)/shard_map/all_gather | solution.py:35
  590.3 20.0 %fusion.1 = bf16[1,768,1024]{1,2,0:T(8,128)(2,1)} fusion(bf16[8192,1024]{1,0:T(8,128)(2,1)} %bitcast.11, bf16[768,8192]{1,0:T(8,128)(2,1)} %all-gather.2.cloned.1.call-done), kind=kOutput, calls=%fused_computation.10 | convolution fusion | flops 12885688320 | bytes 30932992 | tf_op jit(solution)/shard_map/dot_general | solution.py:45
  610.3 188.0 %all-to-all-done = bf16[16,512,1024]{2,1,0:T(8,128)(2,1)} async-done(((bf16[16,512,1024]{2,1,0:T(8,128)(2,1)}), bf16[16,512,1024]{2,1,0:T(8,128)(2,1)}, u32[]{:S(2)}, u32[]{:S(2)}) %all-to-all-start) | async-done | bytes 16777248 | tf_op jit(solution)/shard_map/all_to_all | solution.py:11
  798.3 0.0 copy-start.1
  798.3 19.0 %fusion = bf16[1,768,1024]{1,2,0:T(8,128)(2,1)S(1)} fusion(bf16[8192,1024]{1,0:T(8,128)(2,1)} %bitcast.4, bf16[768,8192]{1,0:T(8,128)(2,1)} %all-gather.2.cloned.1.call-done), kind=kOutput, calls=%fused_computation.9 | convolution fusion | flops 12885688320 | bytes 30932992 | tf_op jit(solution)/shard_map/dot_general | solution.py:45
  817.3 0.0 copy-done.1
  817.3 0.3 pad_maximum_fusion
  817.6 2.9 copy.6
  (2 shorter events, 0.0 us)
Async XLA Ops:
  6.5 3.3 copy-start.2
  6.5 3.3 copy-start.3
  6.5 3.3 copy-start
  6.5 3.7 copy-start.4
  54.2 369.1 %all-to-all-start.1 = ((bf16[16,512,1024]{2,1,0:T(8,128)(2,1)}), bf16[16,512,1024]{2,1,0:T(8,128)(2,1)}, u32[]{:S(2)}, u32[]{:S(2)}) async-start(bf16[16,512,1024]{2,1,0:T(8,128)(2,1)} %stack.12), calls=%async_computation.1 | async-start | bytes 33554432 | tf_op jit(solution)/shard_map/all_to_all | solution.py:11
  429.2 369.1 %all-to-all-start = ((bf16[16,512,1024]{2,1,0:T(8,128)(2,1)}), bf16[16,512,1024]{2,1,0:T(8,128)(2,1)}, u32[]{:S(2)}, u32[]{:S(2)}) async-start(bf16[16,512,1024]{2,1,0:T(8,128)(2,1)} %stack.10), calls=%async_computation | async-start | bytes 33554432 | tf_op jit(solution)/shard_map/all_to_all | solution.py:11
  434.3 155.9 %all-gather.2.cloned.1.call-start = ((), (), s32[]{:S(2)}) async-start(), calls=%async_computation.2 | async-start | bytes 18874368 | tf_op jit(solution)/shard_map/all_gather | solution.py:35
  798.3 19.0 %copy-start.1 = (bf16[1,768,1024]{1,2,0:T(8,128)(2,1)S(1)}, bf16[1,768,1024]{1,2,0:T(8,128)(2,1)}, u32[]{:S(2)}) copy-start(bf16[1,768,1024]{1,2,0:T(8,128)(2,1)} %fusion.1) | copy-start | bytes 4718596
Sparse Core Ops, SparseCore 0:
  436.7 153.5 all-gather.1
